TPU v7x, 32 devices: a whole 2x2x4 slice. The times are simulated.
32 devices in a mesh: grp: 2 (over y), lon: 4 (over x, core), lat: 4 (over z).
Axes of the slice: x: 2, y: 2, z: 4, core: 2. Of those that a mesh axis runs over, the one named last changes fastest.
Arguments:
- tracers: float32 [4, 64, 128, 128], P('grp', 'lat', 'lon'), parts along dimension 0, may hold values from -6 to 6
- adjoint_in: float32 [4, 64, 128, 128], P('grp', 'lat', 'lon'), parts along dimension 0, may hold values from -6 to 6
- shifts: int32 [2, 64], replicated, may hold values from 0 to 127, as said below
- fractions: float32 [2, 64], replicated, may hold values from 0.05 to 0.95
- meridional: float32 [2, 64, 128], P(None, None, 'lon'), may hold values from -0.9 to 0.9
Outputs:
- advected: float32 [4, 64, 128, 128], P('grp', 'lat', 'lon'), parts along dimension 0
- adjoint_out: float32 [4, 64, 128, 128], P('grp', 'lat', 'lon'), parts along dimension 0
There are 2 independent parts, one for each index of `grp`. A program takes and returns all parts, laid end to end along the dimension named above; an argument that names none is the same for every part. Nothing has to cross between parts.
Inputs may be any that keep to these rules, and one draw needn't show every extreme that they name: At row j, shifts lie below 1 + (127) d^2 / 63^2 with d = |2j - 63|.
All inputs are finite; a program needn't handle non-finite values.
Results may differ from a plain program's by a relative error of at most 0.0003.
Values sent between devices are 32-bit elements; how exact they have to be, the bound alone decides.
A program may use at most 128 MiB of HBM per device.

v0:
```python
import jax
import jax.numpy as jnp
from jax import lax
from jax.sharding import PartitionSpec as P


def shifted_2(value, axis, steps):
    count = lax.axis_size(axis)
    pairs = [(source, (source + steps) % count) for source in range(count)]
    return lax.ppermute(value, axis, pairs)


def extended_2(x, sides, width, wrap):
    for axis, dim in sides:
        size, length = (lax.axis_size(axis), x.shape[dim])
        up = [(i, (i + 1) % size) for i in range(size if wrap else size - 1)]
        down = [(j, i) for i, j in up]
        last = lax.slice_in_dim(x, length - width, length, axis=dim)
        first = lax.slice_in_dim(x, 0, width, axis=dim)
        before = lax.ppermute(last, axis, up)
        after = lax.ppermute(first, axis, down)
        x = jnp.concatenate([before, x, after], axis=dim)
    return x


def take_slice(values_in, start_at, stop_at, dimension):
    return lax.slice_in_dim(values_in, start_at, stop_at, axis=dimension)


def edge_values(values_in, amount, dimension):
    inner_sum = take_slice(values_in, 1, amount + 1, dimension) + take_slice(
        values_in, 2, amount + 2, dimension
    )
    outer_sum = take_slice(values_in, 0, amount, dimension) + take_slice(
        values_in, 3, amount + 3, dimension
    )
    return (7.0 * inner_sum - outer_sum) / 12.0


def cell_profile(values_in, dimension):
    interior = values_in.shape[dimension] - 6
    edge_row = edge_values(values_in, interior + 3, dimension)
    left_edge = take_slice(edge_row, 0, interior + 2, dimension)
    right_edge = take_slice(edge_row, 1, interior + 3, dimension)
    centres = take_slice(values_in, 2, interior + 4, dimension)
    curvature = 6.0 * centres - 3.0 * (left_edge + right_edge)
    return (interior, left_edge, right_edge, right_edge - left_edge, curvature)


def zonal_step(values_in, courant, dimension):
    interior, left_edge, right_edge, difference, curvature = cell_profile(values_in, dimension)
    transport = courant * (
        right_edge - 0.5 * courant * (difference - (1.0 - courant * (2.0 / 3.0)) * curvature)
    )
    return (
        take_slice(values_in, 3, interior + 3, dimension)
        - take_slice(transport, 1, interior + 1, dimension)
        + take_slice(transport, 0, interior, dimension)
    )


def meridional_step(values_in, face_courant, dimension):
    interior, left_edge, right_edge, difference, curvature = cell_profile(values_in, dimension)

    def below_part(source):
        return take_slice(source, 0, interior + 1, dimension)

    def above_part(source):
        return take_slice(source, 1, interior + 2, dimension)

    northward = face_courant * (
        below_part(right_edge)
        - 0.5
        * face_courant
        * (below_part(difference) - (1.0 - face_courant * (2.0 / 3.0)) * below_part(curvature))
    )
    southward = face_courant * (
        above_part(left_edge)
        - 0.5 * face_courant * above_part(difference)
        - above_part(curvature) * (0.5 * face_courant + face_courant * face_courant / 3.0)
    )
    transport = jnp.where(face_courant > 0.0, northward, southward)
    return (
        take_slice(values_in, 3, interior + 3, dimension)
        - take_slice(transport, 1, interior + 1, dimension)
        + take_slice(transport, 0, interior, dimension)
    )


def pick_window(joined, offsets, length):

    def one_row(row_values, row_offset):
        return lax.dynamic_slice_in_dim(row_values, row_offset, length, 0)

    return jax.vmap(jax.vmap(one_row))(joined, offsets)


def fetch_doubling(extended, shift_rows, margin):
    cell_count = extended.shape[2] - 2 * margin
    whole_blocks = shift_rows // cell_count
    offsets = cell_count - shift_rows % cell_count
    current = extended
    for bit_number in range((lax.axis_size("lon") - 1).bit_length()):
        moved = shifted_2(current, "lon", 1 << bit_number)
        chosen = jnp.right_shift(whole_blocks, bit_number) % 2 == 1
        current = jnp.where(chosen[:, :, None, None], moved, current)
    previous = shifted_2(current, "lon", 1)
    joined = jnp.concatenate([previous[:, :, :cell_count], current], axis=2)
    return pick_window(joined, offsets, cell_count + 2 * margin)


def zonal_transpose(rimmed_adjoint, courant, cell_count):
    level_count, row_count, _, tracer_count = rimmed_adjoint.shape
    zonal_placeholder = jnp.zeros(
        (level_count, row_count, cell_count + 12, tracer_count), jnp.float32
    )

    def zonal_only(values_in):
        return zonal_step(values_in, courant, 2)

    _, zonal_pullback = jax.vjp(zonal_only, zonal_placeholder)
    return zonal_pullback(rimmed_adjoint)[0][:, :, 6 : 6 + cell_count]


def local(tracers, adjoint_in, shifts, fractions, meridional):
    level_count, row_count, cell_count, tracer_count = tracers.shape
    total_cells = cell_count * lax.axis_size("lon")
    total_rows = shifts.shape[1]
    first_row = lax.axis_index("lat") * row_count
    my_shifts = lax.dynamic_slice_in_dim(shifts, first_row, row_count, 1)
    my_fractions = lax.dynamic_slice_in_dim(fractions, first_row, row_count, 1)[:, :, None, None]
    row_ids = jnp.arange(total_rows, dtype=jnp.int32)[None, :, None]
    face_values = jnp.where(row_ids > 0, meridional, 0.0)
    padded_faces = jnp.pad(face_values, ((0, 0), (3, 4), (0, 0)))
    own_faces = lax.dynamic_slice_in_dim(padded_faces, first_row + 3, row_count + 1, 1)[..., None]
    rimmed = extended_2(tracers, (("lon", 2),), 3, True)
    shifted = fetch_doubling(rimmed, my_shifts, 3)
    zonal = zonal_step(shifted, my_fractions, 2)
    banded = extended_2(zonal, (("lat", 1),), 3, False)
    advected = meridional_step(banded, own_faces, 1)
    widened = extended_2(adjoint_in, (("lat", 1),), 3, False)
    wide_faces = lax.dynamic_slice_in_dim(padded_faces, first_row, row_count + 7, 1)[..., None]
    placeholder = jnp.zeros((level_count, row_count + 12, cell_count, tracer_count), jnp.float32)

    def wide_sweep(values_in):
        return meridional_step(values_in, wide_faces, 1)

    _, pullback = jax.vjp(wide_sweep, placeholder)
    spread = pullback(widened)[0]
    pulled = spread[:, 6 : 6 + row_count]
    back_shifts = jnp.mod(total_cells - my_shifts, total_cells)
    rimmed_adjoint = extended_2(pulled, (("lon", 2),), 3, True)
    transposed = zonal_transpose(rimmed_adjoint, my_fractions, cell_count)
    adjoint_out = fetch_doubling(transposed, back_shifts, 0)
    return (advected, adjoint_out)


def solution(mesh):
    in_specs = (
        P("grp", "lat", "lon", None),
        P("grp", "lat", "lon", None),
        P(),
        P(),
        P(None, None, "lon"),
    )
    out_specs = (P("grp", "lat", "lon", None), P("grp", "lat", "lon", None))
    return jax.shard_map(local, mesh=mesh, in_specs=in_specs, out_specs=out_specs, check_vma=False)
```

profile of v0, /device:TPU:0, one launch (start us, length us, event | category | flops | bytes accessed | tf_op | source)
XLA Modules:
  0.0 81.9 jit_solution(2097422884957183865)
XLA Ops:
  0.7 1.4 %copy.40 = f32[2,16,32,128]{3,1,0,2:T(8,128)S(1)} copy(f32[2,16,32,128]{3,2,1,0:T(8,128)} %param.6) | data formatting | bytes 1048576 | tf_op args[1]
  2.1 5.0 %collective-permute-start.7 = (f32[2,3,32,128]{3,1,0,2:T(4,128)S(1)}, f32[2,3,32,128]{3,1,0,2:T(4,128)S(1)}, u32[]{:S(2)}, u32[]{:S(2)}) collective-permute-start(f32[2,3,32,128]{3,1,0,2:T(4,128)S(1)} %get-tuple-element.47), channel_id=1, source_target_pairs={{0,1},{1,2},{2,3},{4,5},{5,6},{6,7},{8,9},{9,10},{10,11},{12,13},{... | collective-permute-start | bytes 294920 | tf_op jit(solution)/shard_map/ppermute | solution.py:20
  7.1 1.3 %collective-permute-start.8 = (f32[2,3,32,128]{3,1,0,2:T(4,128)S(1)}, f32[2,3,32,128]{3,1,0,2:T(4,128)S(1)}, u32[]{:S(2)}, u32[]{:S(2)}) collective-permute-start(f32[2,3,32,128]{3,1,0,2:T(4,128)S(1)} %get-tuple-element.48), channel_id=1, source_target_pairs={{1,0},{2,1},{3,2},{5,4},{6,5},{7,6},{9,8},{10,9},{11,10},{13,12},{... | collective-permute-start | bytes 294920 | tf_op jit(solution)/shard_map/ppermute | solution.py:21
  8.5 0.1 collective-permute-start
  8.5 1.7 %collective-permute-start.1 = (f32[2,16,3,128]{3,1,0,2:T(8,128)S(1)}, f32[2,16,3,128]{3,1,0,2:T(8,128)S(1)}, u32[]{:S(2)}, u32[]{:S(2)}) collective-permute-start(f32[2,16,3,128]{3,1,0,2:T(8,128)S(1)} %copy.83), channel_id=1, source_target_pairs={{4,0},{8,4},{12,8},{0,12},{5,1},{9,5},{13,9},{1,13},{6,2},{10,6},{... | collective-permute-start | bytes 147464 | tf_op jit(solution)/shard_map/ppermute | solution.py:21
  10.3 0.1 copy.39
  10.4 0.1 broadcast_select_fusion.4
  10.5 0.1 broadcast_multiply_fusion.4
  10.6 0.1 fusion.37
  10.7 0.1 fusion.36
  10.8 0.1 copy.43
  10.9 0.1 copy.47
  11.0 0.1 copy.46
  11.1 0.1 copy.44
  11.2 0.1 copy.45
  11.3 0.7 collective-permute-done
  12.0 0.3 constant_dynamic-update-slice_fusion.1
  12.4 1.6 %collective-permute-start.2 = (f32[2,16,38,128]{3,1,0,2:T(8,128)S(1)}, f32[2,16,38,128]{3,1,0,2:T(8,128)S(1)}, u32[]{:S(2)}, u32[]{:S(2)}) collective-permute-start(f32[2,16,38,128]{3,1,0,2:T(8,128)S(1)} %constant_dynamic-update-slice_fusion), channel_id=1, source_target_pairs={{0,4},{4,8},{8,12},{12,0},{1,5},{5,9},{9,13},{13,1},{2,6},{6,10},{... | collective-permute-start | bytes 1867784 | tf_op jit(solution)/shard_map/ppermute | solution.py:10
  14.0 0.2 pad_maximum_fusion.2
  14.1 1.3 %negate_multiply_fusion.1 = (f32[2,23,32,128]{3,1,0,2:T(8,128)S(1)}, f32[2,23,32,128]{3,1,0,2:T(8,128)S(1)}, f32[2,23,32,128]{3,1,0,2:T(8,128)S(1)}, f32[2,23,32,128]{3,1,0,2:T(8,128)S(1)}, f32[2,23,32,128]{3,1,0,2:T(8,128)S(1)}) fusion(f32[2,23,32]{1,0,2:T(2,128)S(1)} %copy.46, f32[2,23,32]{1,0,2:T(2,128)S(1)} %copy.47, ...), kind=kLoop, calls=%fused_computation.13 | loop fusion | flops 2072576 | bytes 5235136 | tf_op jit(solution)/shard_map/transpose(jvp())/mul | solution.py:75
  15.5 0.3 negate_multiply_fusion.3
  15.8 0.5 add_add_fusion.1
  16.2 0.3 multiply_negate_fusion
  16.5 0.1 pad_add_fusion.12
  16.6 0.3 collective-permute-start.10
  16.9 0.3 collective-permute-start.9
  17.2 0.5 pad_add_fusion
  17.7 0.1 slice.182
  17.8 1.2 %collective-permute-done.10 = f32[2,16,3,128]{3,1,0,2:T(8,128)S(1)} collective-permute-done((f32[2,16,3,128]{3,1,0,2:T(8,128)S(1)}, f32[2,16,3,128]{3,1,0,2:T(8,128)S(1)}, u32[]{:S(2)}, u32[]{:S(2)}) %collective-permute-start.10) | collective-permute-done | bytes 49184 | tf_op jit(solution)/shard_map/ppermute | solution.py:21
  19.0 4.1 %collective-permute-done.9 = f32[2,16,3,128]{3,1,0,2:T(8,128)S(1)} collective-permute-done((f32[2,16,3,128]{3,1,0,2:T(8,128)S(1)}, f32[2,16,3,128]{3,1,0,2:T(8,128)S(1)}, u32[]{:S(2)}, u32[]{:S(2)}) %collective-permute-start.9) | collective-permute-done | bytes 49184 | tf_op jit(solution)/shard_map/ppermute | solution.py:20
  23.1 0.1 pad_maximum_fusion.4
  23.3 0.4 multiply_multiply_fusion
  23.7 0.2 multiply_negate_fusion.1
  23.8 0.2 pad_add_fusion.6
  24.2 0.2 broadcast_select_fusion
  24.3 1.6 %collective-permute-start.3 = (f32[2,16,38,128]{3,1,0,2:T(8,128)S(1)}, f32[2,16,38,128]{3,1,0,2:T(8,128)S(1)}, u32[]{:S(2)}, u32[]{:S(2)}) collective-permute-start(f32[2,16,38,128]{3,1,0,2:T(8,128)S(1)} %broadcast_select_fusion), channel_id=1, source_target_pairs={{0,8},{4,12},{8,0},{12,4},{1,9},{5,13},{9,1},{13,5},{2,10},{6,14},... | collective-permute-start | bytes 1867784 | tf_op jit(solution)/shard_map/ppermute | solution.py:10
  25.9 11.6 %collective-permute-done.11 = f32[2,16,32,128]{3,1,0,2:T(8,128)S(1)} collective-permute-done((f32[2,16,32,128]{3,1,0,2:T(8,128)S(1)}, f32[2,16,32,128]{3,1,0,2:T(8,128)S(1)}, u32[]{:S(2)}, u32[]{:S(2)}) %collective-permute-start.11) | collective-permute-done | bytes 524320 | tf_op jit(solution)/shard_map/ppermute | solution.py:10
  37.5 0.1 broadcast_select_fusion.2
  37.7 1.6 %collective-permute-start.12 = (f32[2,16,32,128]{3,1,0,2:T(8,128)S(1)}, f32[2,16,32,128]{3,1,0,2:T(8,128)S(1)}, u32[]{:S(2)}, u32[]{:S(2)}) collective-permute-start(f32[2,16,32,128]{3,1,0,2:T(8,128)S(1)} %broadcast_select_fusion.2), channel_id=1, source_target_pairs={{0,8},{4,12},{8,0},{12,4},{1,9},{5,13},{9,1},{13,5},{2,10},{6,14},... | collective-permute-start | bytes 1572872 | tf_op jit(solution)/shard_map/ppermute | solution.py:10
  39.2 2.0 %collective-permute-done.3 = f32[2,16,38,128]{3,1,0,2:T(8,128)S(1)} collective-permute-done((f32[2,16,38,128]{3,1,0,2:T(8,128)S(1)}, f32[2,16,38,128]{3,1,0,2:T(8,128)S(1)}, u32[]{:S(2)}, u32[]{:S(2)}) %collective-permute-start.3) | collective-permute-done | bytes 622624 | tf_op jit(solution)/shard_map/ppermute | solution.py:10
  41.3 0.2 broadcast_select_fusion.1
  41.5 9.7 %collective-permute-start.4 = (f32[2,16,38,128]{3,1,0,2:T(8,128)S(1)}, f32[2,16,38,128]{3,1,0,2:T(8,128)S(1)}, u32[]{:S(2)}, u32[]{:S(2)}) collective-permute-start(f32[2,16,38,128]{3,1,0,2:T(8,128)S(1)} %broadcast_select_fusion.1), channel_id=1, source_target_pairs={{0,4},{4,8},{8,12},{12,0},{1,5},{5,9},{9,13},{13,1},{2,6},{6,10},{... | collective-permute-start | bytes 1867784 | tf_op jit(solution)/shard_map/ppermute | solution.py:10
  51.2 0.1 reshape.49
  51.3 0.1 reshape.43
  51.4 1.2 %collective-permute-done.12 = f32[2,16,32,128]{3,1,0,2:T(8,128)S(1)} collective-permute-done((f32[2,16,32,128]{3,1,0,2:T(8,128)S(1)}, f32[2,16,32,128]{3,1,0,2:T(8,128)S(1)}, u32[]{:S(2)}, u32[]{:S(2)}) %collective-permute-start.12) | collective-permute-done | bytes 524320 | tf_op jit(solution)/shard_map/ppermute | solution.py:10
  52.5 0.1 broadcast_select_fusion.3
  52.7 4.6 %collective-permute-start.13 = (f32[2,16,32,128]{3,1,0,2:T(8,128)S(1)}, f32[2,16,32,128]{3,1,0,2:T(8,128)S(1)}, u32[]{:S(2)}, u32[]{:S(2)}) collective-permute-start(f32[2,16,32,128]{3,1,0,2:T(8,128)S(1)} %broadcast_select_fusion.3), channel_id=1, source_target_pairs={{0,4},{4,8},{8,12},{12,0},{1,5},{5,9},{9,13},{13,1},{2,6},{6,10},{... | collective-permute-start | bytes 1572872 | tf_op jit(solution)/shard_map/ppermute | solution.py:10
  57.3 6.6 %collective-permute-done.4 = f32[2,16,38,128]{3,1,0,2:T(8,128)S(1)} collective-permute-done((f32[2,16,38,128]{3,1,0,2:T(8,128)S(1)}, f32[2,16,38,128]{3,1,0,2:T(8,128)S(1)}, u32[]{:S(2)}, u32[]{:S(2)}) %collective-permute-start.4) | collective-permute-done | bytes 622624 | tf_op jit(solution)/shard_map/ppermute | solution.py:10
  64.0 0.1 pad_maximum_fusion
  64.1 1.8 %gather_fusion = f32[32,38,128]{2,0,1:T(8,128)S(1)} fusion(f32[2,16,70,128]{3,1,0,2:T(8,128)S(1)} %pad_maximum_fusion, s32[32]{0:T(128)S(1)} %reshape.43), kind=kCustom, calls=%fused_computation | custom fusion | bytes 1245696 | tf_op jit(solution)/shard_map/vmap(vmap())/gather | solution.py:93
  66.0 0.3 fusion.43
  66.3 1.3 %fusion.7 = f32[2,16,35,128]{3,2,1,0:T(8,128)S(1)} fusion(f32[2,16,35,128]{3,1,0,2:T(8,128)S(1)} %get-tuple-element.44, f32[2,16,35,128]{3,1,0,2:T(8,128)S(1)} %get-tuple-element.45, f32[2,16,35,128]{3,1,0,2:T(8,128)S(1)} %get-tuple-element.46, f32[2,16,35,128]{3,1,0,2:T(8,128)S(1)} %get-tuple-element.43), kind=kLoop, calls=%fused_computation.32 | loop fusion | flops 716800 | bytes 2867200 | tf_op jit(solution)/shard_map/div | solution.py:37
  67.6 0.6 fusion.5
  68.3 0.3 slice_add_fusion.2
  68.6 4.6 %collective-permute-start.5 = (f32[2,3,32,128]{3,2,1,0:T(8,128)S(1)}, f32[2,3,32,128]{3,2,1,0:T(8,128)S(1)}, u32[]{:S(2)}, u32[]{:S(2)}) collective-permute-start(f32[2,3,32,128]{3,2,1,0:T(8,128)S(1)} %get-tuple-element.49), channel_id=1, source_target_pairs={{0,1},{1,2},{2,3},{4,5},{5,6},{6,7},{8,9},{9,10},{10,11},{12,13},{... | collective-permute-start | bytes 294920 | tf_op jit(solution)/shard_map/ppermute | solution.py:20
  73.2 1.3 %collective-permute-start.6 = (f32[2,3,32,128]{3,2,1,0:T(8,128)S(1)}, f32[2,3,32,128]{3,2,1,0:T(8,128)S(1)}, u32[]{:S(2)}, u32[]{:S(2)}) collective-permute-start(f32[2,3,32,128]{3,2,1,0:T(8,128)S(1)} %get-tuple-element.50), channel_id=1, source_target_pairs={{1,0},{2,1},{3,2},{5,4},{6,5},{7,6},{9,8},{10,9},{11,10},{13,12},{... | collective-permute-start | bytes 294920 | tf_op jit(solution)/shard_map/ppermute | solution.py:21
  74.5 0.1 pad_maximum_fusion.1
  74.6 1.6 %gather_fusion.1 = f32[32,32,128]{2,0,1:T(8,128)S(1)} fusion(f32[2,16,64,128]{3,1,0,2:T(8,128)S(1)} %pad_maximum_fusion.1, s32[32]{0:T(128)S(1)} %reshape.49), kind=kCustom, calls=%fused_computation.1 | custom fusion | bytes 1049088 | tf_op jit(solution)/shard_map/vmap(vmap())/gather | solution.py:93
  76.2 1.1 %copy.48 = f32[2,16,32,128]{3,2,1,0:T(8,128)} copy(f32[2,16,32,128]{3,1,0,2:T(8,128)S(1)} %bitcast.17) | data formatting | bytes 1048576
  77.3 2.4 %collective-permute-done.6 = f32[2,3,32,128]{3,2,1,0:T(8,128)S(1)} collective-permute-done((f32[2,3,32,128]{3,2,1,0:T(8,128)S(1)}, f32[2,3,32,128]{3,2,1,0:T(8,128)S(1)}, u32[]{:S(2)}, u32[]{:S(2)}) %collective-permute-start.6) | collective-permute-done | bytes 98336 | tf_op jit(solution)/shard_map/ppermute | solution.py:21
  79.7 0.2 fusion.12
  79.9 0.2 slice_subtract_fusion
  80.1 0.9 %fusion.18 = f32[2,17,32,128]{3,2,1,0:T(8,128)S(1)} fusion(f32[2,18,32,128]{3,2,1,0:T(8,128)S(1)} %get-tuple-element.42, f32[2,18,32,128]{3,2,1,0:T(8,128)S(1)} %get-tuple-element.41, f32[2,19,32,128]{3,2,1,0:T(8,128)S(1)} %fusion.12, f32[2,17,32]{2,1,0:T(8,128)S(1)} %get-tuple-element.57, f32[2,17,32]{2,1,0:T(8,128)S(1)} %get-tuple-element.56, ...), kind=kLoop, calls=%fused_computation.54 | loop fusion | flops 1531904 | bytes 3360832 | tf_op jit(solution)/shard_map/jit(_where)/select_n | solution.py:82
  81.0 0.9 %slice_add_fusion.1 = f32[2,16,32,128]{3,2,1,0:T(8,128)} fusion(f32[2,17,32,128]{3,2,1,0:T(8,128)S(1)} %fusion.18, f32[2,16,32,128]{3,2,1,0:T(8,128)S(1)} %slice_add_fusion.2), kind=kLoop, calls=%fused_computation.68 | loop fusion | flops 262144 | bytes 2097152 | tf_op jit(solution)/shard_map/add | solution.py:84
  (36 shorter events, 0.5 us)
Async XLA Ops:
  0.6 7.8 %copy-start = (f32[2,16,32,128]{3,2,1,0:T(8,128)S(1)}, f32[2,16,32,128]{3,2,1,0:T(8,128)}, u32[]{:S(2)}) copy-start(f32[2,16,32,128]{3,2,1,0:T(8,128)} %param.5) | copy-start | bytes 1572868
  0.6 9.6 %copy-start.1 = (f32[2,64,32]{1,2,0:T(8,128)S(1)}, f32[2,64,32]{1,2,0:T(8,128)}, u32[]{:S(2)}) copy-start(f32[2,64,32]{1,2,0:T(8,128)} %param.9) | copy-start | bytes 49156
  0.7 9.8 %copy-start.3 = (f32[2,64]{1,0:T(2,128)S(1)}, f32[2,64]{1,0:T(2,128)}, u32[]{:S(2)}) copy-start(f32[2,64]{1,0:T(2,128)} %param.8) | copy-start | bytes 1540
  0.7 9.9 %copy-start.2 = (s32[2,64]{1,0:T(2,128)S(1)}, s32[2,64]{1,0:T(2,128)}, u32[]{:S(2)}) copy-start(s32[2,64]{1,0:T(2,128)} %param.7) | copy-start | bytes 1540
  2.1 11.8 %collective-permute-start.7 = (f32[2,3,32,128]{3,1,0,2:T(4,128)S(1)}, f32[2,3,32,128]{3,1,0,2:T(4,128)S(1)}, u32[]{:S(2)}, u32[]{:S(2)}) collective-permute-start(f32[2,3,32,128]{3,1,0,2:T(4,128)S(1)} %get-tuple-element.47), channel_id=1, source_target_pairs={{0,1},{1,2},{2,3},{4,5},{5,6},{6,7},{8,9},{9,10},{10,11},{12,13},{... | collective-permute-start | bytes 294920 | tf_op jit(solution)/shard_map/ppermute | solution.py:20
  7.1 6.9 %collective-permute-start.8 = (f32[2,3,32,128]{3,1,0,2:T(4,128)S(1)}, f32[2,3,32,128]{3,1,0,2:T(4,128)S(1)}, u32[]{:S(2)}, u32[]{:S(2)}) collective-permute-start(f32[2,3,32,128]{3,1,0,2:T(4,128)S(1)} %get-tuple-element.48), channel_id=1, source_target_pairs={{1,0},{2,1},{3,2},{5,4},{6,5},{7,6},{9,8},{10,9},{11,10},{13,12},{... | collective-permute-start | bytes 294920 | tf_op jit(solution)/shard_map/ppermute | solution.py:21
  8.5 3.6 %collective-permute-start = (f32[2,16,3,128]{3,1,0,2:T(8,128)S(1)}, f32[2,16,3,128]{3,1,0,2:T(8,128)S(1)}, u32[]{:S(2)}, u32[]{:S(2)}) collective-permute-start(f32[2,16,3,128]{3,1,0,2:T(8,128)S(1)} %copy.82), channel_id=1, source_target_pairs={{0,4},{4,8},{8,12},{12,0},{1,5},{5,9},{9,13},{13,1},{2,6},{6,10},{... | collective-permute-start | bytes 147464 | tf_op jit(solution)/shard_map/ppermute | solution.py:20
  8.5 3.8 %collective-permute-start.1 = (f32[2,16,3,128]{3,1,0,2:T(8,128)S(1)}, f32[2,16,3,128]{3,1,0,2:T(8,128)S(1)}, u32[]{:S(2)}, u32[]{:S(2)}) collective-permute-start(f32[2,16,3,128]{3,1,0,2:T(8,128)S(1)} %copy.83), channel_id=1, source_target_pairs={{4,0},{8,4},{12,8},{0,12},{5,1},{9,5},{13,9},{1,13},{6,2},{10,6},{... | collective-permute-start | bytes 147464 | tf_op jit(solution)/shard_map/ppermute | solution.py:21
  12.4 11.8 %collective-permute-start.2 = (f32[2,16,38,128]{3,1,0,2:T(8,128)S(1)}, f32[2,16,38,128]{3,1,0,2:T(8,128)S(1)}, u32[]{:S(2)}, u32[]{:S(2)}) collective-permute-start(f32[2,16,38,128]{3,1,0,2:T(8,128)S(1)} %constant_dynamic-update-slice_fusion), channel_id=1, source_target_pairs={{0,4},{4,8},{8,12},{12,0},{1,5},{5,9},{9,13},{13,1},{2,6},{6,10},{... | collective-permute-start | bytes 1867784 | tf_op jit(solution)/shard_map/ppermute | solution.py:10
  16.6 2.4 %collective-permute-start.10 = (f32[2,16,3,128]{3,1,0,2:T(8,128)S(1)}, f32[2,16,3,128]{3,1,0,2:T(8,128)S(1)}, u32[]{:S(2)}, u32[]{:S(2)}) collective-permute-start(f32[2,16,3,128]{3,1,0,2:T(8,128)S(1)} %get-tuple-element.24), channel_id=1, source_target_pairs={{4,0},{8,4},{12,8},{0,12},{5,1},{9,5},{13,9},{1,13},{6,2},{10,6},{... | collective-permute-start | bytes 147464 | tf_op jit(solution)/shard_map/ppermute | solution.py:21
  16.9 6.3 %collective-permute-start.9 = (f32[2,16,3,128]{3,1,0,2:T(8,128)S(1)}, f32[2,16,3,128]{3,1,0,2:T(8,128)S(1)}, u32[]{:S(2)}, u32[]{:S(2)}) collective-permute-start(f32[2,16,3,128]{3,1,0,2:T(8,128)S(1)} %get-tuple-element.23), channel_id=1, source_target_pairs={{0,4},{4,8},{8,12},{12,0},{1,5},{5,9},{9,13},{13,1},{2,6},{6,10},{... | collective-permute-start | bytes 147464 | tf_op jit(solution)/shard_map/ppermute | solution.py:20
  24.1 13.4 %collective-permute-start.11 = (f32[2,16,32,128]{3,1,0,2:T(8,128)S(1)}, f32[2,16,32,128]{3,1,0,2:T(8,128)S(1)}, u32[]{:S(2)}, u32[]{:S(2)}) collective-permute-start(f32[2,16,32,128]{3,1,0,2:T(8,128)S(1)} %pad_add_fusion.6), channel_id=1, source_target_pairs={{0,4},{4,8},{8,12},{12,0},{1,5},{5,9},{9,13},{13,1},{2,6},{6,10},{... | collective-permute-start | bytes 1572872 | tf_op jit(solution)/shard_map/ppermute | solution.py:10
  24.3 17.0 %collective-permute-start.3 = (f32[2,16,38,128]{3,1,0,2:T(8,128)S(1)}, f32[2,16,38,128]{3,1,0,2:T(8,128)S(1)}, u32[]{:S(2)}, u32[]{:S(2)}) collective-permute-start(f32[2,16,38,128]{3,1,0,2:T(8,128)S(1)} %broadcast_select_fusion), channel_id=1, source_target_pairs={{0,8},{4,12},{8,0},{12,4},{1,9},{5,13},{9,1},{13,5},{2,10},{6,14},... | collective-permute-start | bytes 1867784 | tf_op jit(solution)/shard_map/ppermute | solution.py:10
  37.7 14.9 %collective-permute-start.12 = (f32[2,16,32,128]{3,1,0,2:T(8,128)S(1)}, f32[2,16,32,128]{3,1,0,2:T(8,128)S(1)}, u32[]{:S(2)}, u32[]{:S(2)}) collective-permute-start(f32[2,16,32,128]{3,1,0,2:T(8,128)S(1)} %broadcast_select_fusion.2), channel_id=1, source_target_pairs={{0,8},{4,12},{8,0},{12,4},{1,9},{5,13},{9,1},{13,5},{2,10},{6,14},... | collective-permute-start | bytes 1572872 | tf_op jit(solution)/shard_map/ppermute | solution.py:10
  41.5 22.5 %collective-permute-start.4 = (f32[2,16,38,128]{3,1,0,2:T(8,128)S(1)}, f32[2,16,38,128]{3,1,0,2:T(8,128)S(1)}, u32[]{:S(2)}, u32[]{:S(2)}) collective-permute-start(f32[2,16,38,128]{3,1,0,2:T(8,128)S(1)} %broadcast_select_fusion.1), channel_id=1, source_target_pairs={{0,4},{4,8},{8,12},{12,0},{1,5},{5,9},{9,13},{13,1},{2,6},{6,10},{... | collective-permute-start | bytes 1867784 | tf_op jit(solution)/shard_map/ppermute | solution.py:10
  52.7 21.8 %collective-permute-start.13 = (f32[2,16,32,128]{3,1,0,2:T(8,128)S(1)}, f32[2,16,32,128]{3,1,0,2:T(8,128)S(1)}, u32[]{:S(2)}, u32[]{:S(2)}) collective-permute-start(f32[2,16,32,128]{3,1,0,2:T(8,128)S(1)} %broadcast_select_fusion.3), channel_id=1, source_target_pairs={{0,4},{4,8},{8,12},{12,0},{1,5},{5,9},{9,13},{13,1},{2,6},{6,10},{... | collective-permute-start | bytes 1572872 | tf_op jit(solution)/shard_map/ppermute | solution.py:10
  68.6 8.7 %collective-permute-start.5 = (f32[2,3,32,128]{3,2,1,0:T(8,128)S(1)}, f32[2,3,32,128]{3,2,1,0:T(8,128)S(1)}, u32[]{:S(2)}, u32[]{:S(2)}) collective-permute-start(f32[2,3,32,128]{3,2,1,0:T(8,128)S(1)} %get-tuple-element.49), channel_id=1, source_target_pairs={{0,1},{1,2},{2,3},{4,5},{5,6},{6,7},{8,9},{9,10},{10,11},{12,13},{... | collective-permute-start | bytes 294920 | tf_op jit(solution)/shard_map/ppermute | solution.py:20
  73.2 6.5 %collective-permute-start.6 = (f32[2,3,32,128]{3,2,1,0:T(8,128)S(1)}, f32[2,3,32,128]{3,2,1,0:T(8,128)S(1)}, u32[]{:S(2)}, u32[]{:S(2)}) collective-permute-start(f32[2,3,32,128]{3,2,1,0:T(8,128)S(1)} %get-tuple-element.50), channel_id=1, source_target_pairs={{1,0},{2,1},{3,2},{5,4},{6,5},{7,6},{9,8},{10,9},{11,10},{13,12},{... | collective-permute-start | bytes 294920 | tf_op jit(solution)/shard_map/ppermute | solution.py:21
where the time goes:
time: 82.1 us; the launch traced here: 81.9 us
  starting transfers between devices  33.6 us (41%)
  waiting for transfers between devices  29.9 us (36%)
  other arithmetic  9.68 us (12%)
  local copies, waits for them, and re-layouts  7.62 us (9%)
  between operations  1.07 us (1%)
    ppermute x6, waiting for transfers between devices, shifted_2(): return lax.ppermute(value, axis, pairs)  21.5 us
    ppermute x6, starting transfers between devices, shifted_2(): return lax.ppermute(value, axis, pairs)  19.1 us
    ppermute x4, starting transfers between devices, extended_2(): before = lax.ppermute(last, axis, up)  9.88 us
    ppermute x4, waiting for transfers between devices, extended_2(): before = lax.ppermute(last, axis, up)  4.85 us
    ppermute x4, starting transfers between devices, extended_2(): after = lax.ppermute(first, axis, down)  4.57 us
    gather x4, local copies, waits for them, and re-layouts, one_row(): return lax.dynamic_slice_in_dim(row_values, row_offset, length, 0)  3.63 us
    ppermute x4, waiting for transfers between devices, extended_2(): after = lax.ppermute(first, axis, down)  3.6 us
    unnamed x15, local copies, waits for them, and re-layouts  2.92 us
  transfers between devices with their start and end apart: 14, of which 8 were waited for; matrix products, arithmetic and copies ran while one was open for 17% of the time, Pallas kernels for 0%

commit v1 on v0

v1 whole, which is shorter than its diff:
```python
import functools

import jax
import jax.numpy as jnp
from jax import lax
from jax.experimental import pallas as pl
from jax.experimental.pallas import tpu as pltpu
from jax.sharding import PartitionSpec as P

MESH = pl.DeviceIdType.MESH
SUB = 8
RIM = 3


def chunk_list(levels, rows, step):
    return [(lv, r0) for lv in range(levels) for r0 in range(0, rows, step)]


def face_terms(v):
    size = jnp.abs(v)
    beta = v * (0.5 * size) * (1.0 - size * (2.0 / 3.0))
    return beta, 0.5 * v * v


def zonal_taps(c):
    b = 1.0 - c * (2.0 / 3.0)
    p = c * (1.0 - 0.5 * c - 1.5 * c * b)
    q = c * (0.5 * c - 1.5 * c * b)
    r = 3.0 * c * c * b
    d = p - q
    t = 1.0 / 12.0
    s = 7.0 / 12.0
    return (
        -t * q,
        s * q - t * d,
        r + t * p + s * d + s * q,
        1.0 - r - s * p + s * d - t * q,
        -s * p - t * d,
        t * p,
    )


def kernel(dims, *refs):
    levels, rows, cells, width, n_lon, n_lat, step = dims
    chunks = chunk_list(levels, rows, step)
    nq = len(chunks)
    tr, ad, shifts, fractions, mer, out_f, out_a = refs[:7]
    gath = (refs[7 : 7 + nq], refs[7 + nq : 7 + 2 * nq])
    zb, ab, vb, taps, of, oa, loc, ssem, rsem, hs, hr, osem = refs[7 + 2 * nq :]
    total_cells = cells * n_lon
    total_rows = rows * n_lat
    n_x = n_lon // 2

    me = lax.axis_index("lon")
    lat = lax.axis_index("lat")
    first = lat * rows
    core = lax.rem(me, 2)
    partner = me + 1 - 2 * core

    own = []
    dup = []
    for q, (lv, r0) in enumerate(chunks):
        a = pltpu.make_async_copy(
            tr.at[lv, pl.ds(r0, step)], gath[0][q].at[:, pl.ds(0, cells)], loc.at[q]
        )
        a.start()
        own.append(a)
    adc = pltpu.make_async_copy(ad, ab.at[:, pl.ds(RIM, rows)], loc.at[2 * nq])
    adc.start()
    for q, (lv, r0) in enumerate(chunks):
        b = pltpu.make_async_copy(
            tr.at[lv, pl.ds(r0, step)],
            gath[0][q].at[:, pl.ds(total_cells, cells)],
            loc.at[nq + q],
        )
        b.start()
        dup.append(b)

    barrier = pltpu.get_barrier_semaphore()
    pl.semaphore_signal(barrier, inc=1, device_id={"lon": partner}, device_id_type=MESH)
    for dx in range(1, n_x):
        pl.semaphore_signal(
            barrier, inc=1, device_id={"lon": lax.rem(me + 2 * dx, n_lon)}, device_id_type=MESH
        )

    @pl.when(lat > 0)
    def _():
        pl.semaphore_signal(barrier, inc=1, device_id={"lat": lat - 1}, device_id_type=MESH)

    @pl.when(lat < n_lat - 1)
    def _():
        pl.semaphore_signal(barrier, inc=1, device_id={"lat": lat + 1}, device_id_type=MESH)

    inner = jnp.logical_and(lat > 0, lat < n_lat - 1)

    @pl.when(inner)
    def _():
        pl.semaphore_wait(barrier, n_x + 2)

    @pl.when(jnp.logical_not(inner))
    def _():
        pl.semaphore_wait(barrier, n_x + min(n_lat - 1, 1))

    def lat_copies(buf, k):
        down = pltpu.make_async_remote_copy(
            buf.at[:, pl.ds(RIM, RIM)],
            buf.at[:, pl.ds(RIM + rows, RIM)],
            hs.at[k, 0],
            hr.at[k, 0],
            device_id={"lat": lat - 1},
            device_id_type=MESH,
        )
        up = pltpu.make_async_remote_copy(
            buf.at[:, pl.ds(rows, RIM)],
            buf.at[:, pl.ds(0, RIM)],
            hs.at[k, 1],
            hr.at[k, 1],
            device_id={"lat": lat + 1},
            device_id_type=MESH,
        )
        return down, up

    def lat_start(buf, k):
        down, up = lat_copies(buf, k)

        @pl.when(lat > 0)
        def _():
            down.start()

        @pl.when(lat < n_lat - 1)
        def _():
            up.start()

    def lat_wait(buf, k):
        down, up = lat_copies(buf, k)

        @pl.when(lat > 0)
        def _():
            down.wait_send()
            up.wait_recv()

        @pl.when(lat < n_lat - 1)
        def _():
            up.wait_send()
            down.wait_recv()

    def x_copy(a, q, dx):
        return pltpu.make_async_remote_copy(
            gath[a][q].at[:, pl.ds(0, cells)],
            gath[a][q].at[:, pl.ds((n_lon - 2 * dx) * cells, cells)],
            ssem.at[a, q, dx],
            rsem.at[a, q, dx],
            device_id={"lon": lax.rem(me + 2 * dx, n_lon)},
            device_id_type=MESH,
        )

    def core_copy(a, q, dx):
        source = ((n_lon - 2 * dx) % n_lon) * cells
        slot = lax.rem(2 * n_lon - 2 * dx + 2 * core - 1, n_lon)
        return pltpu.make_async_remote_copy(
            gath[a][q].at[:, pl.ds(source, cells)],
            gath[a][q].at[:, pl.ds(pl.multiple_of(slot * cells, cells), cells)],
            ssem.at[a, q, n_x + dx],
            rsem.at[a, q, n_x + dx],
            device_id={"lon": partner},
            device_id_type=MESH,
        )

    def gather_start(a, q):
        for dx in range(1, n_x):
            x_copy(a, q, dx).start()
        core_copy(a, q, 0).start()

    def relay(a, q):
        for dx in range(1, n_x):
            x_copy(a, q, dx).wait_recv()
            core_copy(a, q, dx).start()

    def gather_finish(a, q):
        for dx in range(n_x):
            core_copy(a, q, dx).wait_recv()

    def gather_drain(a, q):
        for dx in range(1, n_x):
            x_copy(a, q, dx).wait_send()
        for dx in range(n_x):
            core_copy(a, q, dx).wait_send()

    adc.wait()
    lat_start(ab, 0)
    for q in range(nq):
        own[q].wait()
        gather_start(0, q)

    @pl.when(lat == 0)
    def _():
        for buf in (ab, zb):
            buf[:, pl.ds(0, RIM)] = jnp.zeros((levels, RIM, cells, width), jnp.float32)

    @pl.when(lat == n_lat - 1)
    def _():
        for buf in (ab, zb):
            buf[:, pl.ds(RIM + rows, RIM)] = jnp.zeros((levels, RIM, cells, width), jnp.float32)

    faces = rows + 5
    for lv in range(levels):

        @pl.loop(0, faces)
        def _(f):
            row = first + f - 2
            line = mer[lv, pl.ds(lax.rem(row + total_rows, total_rows), 1), :]
            tall = jnp.broadcast_to(line, (width, cells)).T
            inside = jnp.logical_and(row > 0, row < total_rows)
            vb[lv, f] = jnp.where(inside, tall, 0.0)

        @pl.loop(0, rows)
        def _(r):
            for k, t in enumerate(zonal_taps(fractions[lv, first + r])):
                taps[(lv * rows + r) * 6 + k] = t

    lat_wait(ab, 0)
    for lv in range(levels):

        @pl.loop(0, cells // SUB)
        def _(c):
            at = pl.ds(pl.multiple_of(c * SUB, SUB), SUB)
            ev, q6b, dqb, eb = {}, {}, {}, {}
            carry = None
            y = {r: ab[lv, r + RIM, at, :] for r in range(-3, -1)}
            for f in range(-2, rows + 3):
                y[f] = ab[lv, f + RIM, at, :]
                v = vb[lv, f + 2, at, :]
                north = v > 0.0
                beta, gamma = face_terms(v)
                change = y[f] - y[f - 1]
                ev[f] = v * change
                b = beta * change
                g = -gamma * change
                bn, gn = jnp.where(north, b, 0.0), jnp.where(north, g, 0.0)
                if carry is not None:
                    q6b[f - 1] = bn + carry[0]
                    dqb[f - 1] = gn + carry[1]
                carry = (b - bn, g - gn)
                h = f - 1
                if h >= -1:
                    eb[h] = ev[h] - 3.0 * (q6b[h - 1] + q6b[h]) + (dqb[h - 1] - dqb[h])
                r = h - 2
                if r >= 0:
                    value = (
                        y[r]
                        + 6.0 * q6b[r]
                        + (7.0 / 12.0) * (eb[r] + eb[r + 1])
                        - (1.0 / 12.0) * (eb[r - 1] + eb[r + 2])
                    )
                    q = lv * (rows // step) + r // step
                    gath[1][q][r % step, at, :] = value
                    gath[1][q][
                        r % step, pl.ds(pl.multiple_of(total_cells + c * SUB, SUB), SUB), :
                    ] = value

        for q, (l2, _r) in enumerate(chunks):
            if l2 == lv:
                gather_start(1, q)

    def sweep(a, q, sink, sink_row, sign):
        lv, r0 = chunks[q]
        buf = gath[a][q]

        @pl.loop(0, step)
        def _(r):
            buf[r, pl.ds(total_cells + cells, SUB), :] = buf[r, pl.ds(cells, SUB), :]
            shift = shifts[lv, first + r0 + r]
            if sign < 0:
                start = lax.rem(2 * total_cells - shift - 3, total_cells)
            else:
                start = lax.rem(2 * total_cells + shift - 2, total_cells)
            base = (lv * rows + r0 + r) * 6
            w = [taps[base + k] for k in range(6)]
            if sign > 0:
                w = w[::-1]
            for c in range(cells // SUB):
                total = None
                for k in range(6):
                    term = w[k] * buf[r, pl.ds(start + c * SUB + k, SUB), :]
                    total = term if total is None else total + term
                sink[lv, sink_row + r0 + r, pl.ds(c * SUB, SUB), :] = total

    for b in dup:
        b.wait()
    for q in range(nq):
        relay(0, q)
        if q > 0:
            gather_finish(0, q - 1)
            sweep(0, q - 1, zb, RIM, -1)
    gather_finish(0, nq - 1)
    sweep(0, nq - 1, zb, RIM, -1)
    lat_start(zb, 1)

    relay(1, 0)
    lat_wait(zb, 1)

    for lv in range(levels):

        @pl.loop(0, cells // SUB)
        def _(c):
            at = pl.ds(pl.multiple_of(c * SUB, SUB), SUB)
            z = {r: zb[lv, r + RIM, at, :] for r in range(-3, 0)}
            e, q6, dq, flux = {}, {}, {}, {}
            for f in range(-1, rows + 2):
                z[f + 1] = zb[lv, f + 1 + RIM, at, :]
                e[f] = (7.0 / 12.0) * (z[f - 1] + z[f]) - (1.0 / 12.0) * (z[f - 2] + z[f + 1])
                u = f - 1
                if u >= -1:
                    q6[u] = 6.0 * z[u] - 3.0 * (e[u] + e[f])
                    dq[u] = e[f] - e[u]
                if u >= 0:
                    v = vb[lv, u + 2, at, :]
                    north = v > 0.0
                    beta, gamma = face_terms(v)
                    flux[u] = (
                        v * e[u]
                        + beta * jnp.where(north, q6[u - 1], q6[u])
                        - gamma * jnp.where(north, dq[u - 1], dq[u])
                    )
                if u >= 1:
                    of[lv, u - 1, at, :] = z[u - 1] - flux[u] + flux[u - 1]

    store_f = pltpu.make_async_copy(of, out_f, osem.at[nq])
    store_f.start()

    stores = []

    def finish_adjoint(q):
        lv, r0 = chunks[q]
        gather_finish(1, q)
        sweep(1, q, oa, 0, 1)
        s = pltpu.make_async_copy(
            oa.at[lv, pl.ds(r0, step)], out_a.at[lv, pl.ds(r0, step)], osem.at[q]
        )
        s.start()
        stores.append(s)

    for q in range(1, nq):
        relay(1, q)
        finish_adjoint(q - 1)
    finish_adjoint(nq - 1)

    for a in range(2):
        for q in range(nq):
            gather_drain(a, q)
    store_f.wait()
    for s in stores:
        s.wait()


def local(tracers, adjoint_in, shifts, fractions, meridional):
    levels, rows, cells, width = tracers.shape
    n_lon, n_lat = lax.axis_size("lon"), lax.axis_size("lat")
    step = max(1, rows // 4)
    nq = levels * (rows // step)
    n_x = n_lon // 2
    dims = (levels, rows, cells, width, n_lon, n_lat, step)
    block = pltpu.VMEM((step, (n_lon + 1) * cells + SUB, width), jnp.float32)
    banded = pltpu.VMEM((levels, rows + 2 * RIM, cells, width), jnp.float32)
    whole = pltpu.VMEM((levels, rows, cells, width), jnp.float32)
    anywhere = pl.BlockSpec(memory_space=pl.ANY)
    scalar = pl.BlockSpec(memory_space=pltpu.SMEM)
    shape = jax.ShapeDtypeStruct(tracers.shape, jnp.float32)
    return pl.pallas_call(
        functools.partial(kernel, dims),
        out_shape=(shape, shape),
        in_specs=[anywhere, anywhere, scalar, scalar, pl.BlockSpec(memory_space=pltpu.VMEM)],
        out_specs=(anywhere, anywhere),
        scratch_shapes=[block] * (2 * nq)
        + [
            banded,
            banded,
            pltpu.VMEM((levels, rows + 5, cells, width), jnp.float32),
            pltpu.SMEM((levels * rows * 6,), jnp.float32),
            whole,
            whole,
            pltpu.SemaphoreType.DMA((2 * nq + 1,)),
            pltpu.SemaphoreType.DMA((2, nq, 2 * n_x)),
            pltpu.SemaphoreType.DMA((2, nq, 2 * n_x)),
            pltpu.SemaphoreType.DMA((2, 2)),
            pltpu.SemaphoreType.DMA((2, 2)),
            pltpu.SemaphoreType.DMA((nq + 1,)),
        ],
        compiler_params=pltpu.CompilerParams(
            collective_id=0, has_side_effects=True, vmem_limit_bytes=60 * 1024 * 1024
        ),
    )(tracers, adjoint_in, shifts, fractions, meridional)


def solution(mesh):
    block = P("grp", "lat", "lon", None)
    in_specs = (block, block, P(), P(), P(None, None, "lon"))
    return jax.shard_map(
        local, mesh=mesh, in_specs=in_specs, out_specs=(block, block), check_vma=False
    )
```

time: 82.1 us -> 36.3 us (0.44)
  starting transfers between devices: 33.6 us -> 0 us
  Pallas kernels: 0 us -> 30.9 us
  waiting for transfers between devices: 29.9 us -> 0 us
  other arithmetic: 9.68 us -> 0 us
  local copies, waits for them, and re-layouts: 7.62 us -> 4.19 us
    ppermute x14 -> x0, starting transfers between devices: 33.6 us -> none  [the longest x6 19.1 us: shifted_2(): return lax.ppermute(value, axis, pairs)]
    pallas_call x0 -> x1, Pallas kernels: none -> 30.9 us  [local(): pl.pallas_call(functools.partial(kernel, dims), out_shape=(shape, shape),...]
    ppermute x14 -> x0, waiting for transfers between devices: 29.9 us -> none  [the longest x6 21.5 us: shifted_2(): return lax.ppermute(value, axis, pairs)]
    gather x4 -> x0, local copies, waits for them, and re-layouts: 3.63 us -> none  [one_row(): return lax.dynamic_slice_in_dim(row_values, row_offset, length, 0)]
    mul x7 -> x0, other arithmetic: 2.67 us -> none  [the longest x1 1.35 us: meridional_step(): (1.0 - face_courant * (2.0 / 3.0)) * below_part(curvature)]
    select_n x6 -> x0, other arithmetic: 1.58 us -> none  [the longest x1 0.91 us: meridional_step(): transport = jnp.where(face_courant > 0.0, northward, southward)]
    div x2 -> x0, other arithmetic: 1.47 us -> none  [edge_values(): return (7.0 * inner_sum - outer_sum) / 12.0]
    unnamed x15 -> x5, local copies, waits for them, and re-layouts: 2.92 us -> 4.19 us
  transfers between devices with their start and end apart: 14 -> 0, of which waited for: 8 -> 0; matrix products, arithmetic and copies ran while one was open for 17% -> 0% of each run, Pallas kernels for 0% -> 0%
where the time goes in v1:
time: 36.3 us; the launch traced here: 35.7 us
  Pallas kernels  30.9 us (85%)
  local copies, waits for them, and re-layouts  4.19 us (12%)
  between operations  0.65 us (2%)
    pallas_call x1, Pallas kernels, local(): pl.pallas_call(functools.partial(kernel, dims), out_shape=(shape, shape),...  30.9 us
    unnamed x5, local copies, waits for them, and re-layouts  4.19 us

profile of v1, /device:TPU:0, one launch (start us, length us, event | category | flops | bytes accessed | tf_op | source)
XLA Modules:
  0.0 35.7 jit_solution(13928078951972246986)
XLA Ops:
  0.6 1.5 %copy.7.refs_4_ = f32[2,64,32]{2,1,0:T(8,128)} copy(f32[2,64,32]{1,2,0:T(8,128)} %param.9) | data formatting | bytes 32768 | tf_op args[4]
  2.1 30.9 %shard_map.68 = (f32[2,16,32,128]{3,2,1,0:T(8,128)}, f32[2,16,32,128]{3,2,1,0:T(8,128)}) custom-call(f32[2,16,32,128]{3,2,1,0:T(8,128)} %refs_0_.1, f32[2,16,32,128]{3,2,1,0:T(8,128)} %refs_1_.1, s32[2,64]{1,0:T(2,128)} %refs_2_.1, f32[2,64]{1,0:T(2,128)} %refs_3_.1, f32[2,64,32]{2,1,0:T(8,128)} %copy.7.refs_4_), custom_call_target="tpu_custom_call" | custom-call | tf_op jit(solution)/shard_map/pallas_call | solution.py:369
  33.0 0.0 copy-start
  33.0 1.9 %copy.10 = f32[2,16,32,128]{3,2,1,0:T(8,128)} copy(f32[2,16,32,128]{3,2,1,0:T(8,128)} %get-tuple-element.4) | data formatting | bytes 1048576
  34.9 0.0 copy-done
  34.9 0.8 %copy.11 = f32[2,16,32,128]{3,2,1,0:T(8,128)} copy(f32[2,16,32,128]{3,2,1,0:T(8,128)S(1)} %copy-done) | data formatting | bytes 1048576
Async XLA Ops:
  33.0 1.9 %copy-start = (f32[2,16,32,128]{3,2,1,0:T(8,128)S(1)}, f32[2,16,32,128]{3,2,1,0:T(8,128)}, u32[]{:S(2)}) copy-start(f32[2,16,32,128]{3,2,1,0:T(8,128)} %get-tuple-element.5) | copy-start | bytes 1572868

commit v2 on v1

--- a/solution.py
+++ b/solution.py
@@ -44,9 +44,9 @@
     levels, rows, cells, width, n_lon, n_lat, step = dims
     chunks = chunk_list(levels, rows, step)
     nq = len(chunks)
-    tr, ad, shifts, fractions, mer, out_f, out_a = refs[:7]
+    tr, ad, shifts_in, fractions_in, mer_in, of, oa = refs[:7]
     gath = (refs[7 : 7 + nq], refs[7 + nq : 7 + 2 * nq])
-    zb, ab, vb, taps, of, oa, loc, ssem, rsem, hs, hr, osem = refs[7 + 2 * nq :]
+    zb, ab, vb, taps, shifts, fractions, mer, loc, ssem, rsem, hs, hr = refs[7 + 2 * nq :]
     total_cells = cells * n_lon
     total_rows = rows * n_lat
     n_x = n_lon // 2
@@ -75,6 +75,14 @@
         )
         b.start()
         dup.append(b)
+
+    small = []
+    for k, (source, target) in enumerate(
+        ((shifts_in, shifts), (fractions_in, fractions), (mer_in, mer))
+    ):
+        d = pltpu.make_async_copy(source, target, loc.at[2 * nq + 1 + k])
+        d.start()
+        small.append(d)
 
     barrier = pltpu.get_barrier_semaphore()
     pl.semaphore_signal(barrier, inc=1, device_id={"lon": partner}, device_id_type=MESH)
@@ -202,16 +210,18 @@
         for buf in (ab, zb):
             buf[:, pl.ds(RIM + rows, RIM)] = jnp.zeros((levels, RIM, cells, width), jnp.float32)
 
+    for d in small:
+        d.wait()
     faces = rows + 5
+    lanes = lax.broadcasted_iota(jnp.int32, (cells, total_rows), 1)
     for lv in range(levels):
 
         @pl.loop(0, faces)
         def _(f):
             row = first + f - 2
-            line = mer[lv, pl.ds(lax.rem(row + total_rows, total_rows), 1), :]
-            tall = jnp.broadcast_to(line, (width, cells)).T
-            inside = jnp.logical_and(row > 0, row < total_rows)
-            vb[lv, f] = jnp.where(inside, tall, 0.0)
+            chosen = jnp.logical_and(lanes == row, lanes > 0)
+            column = jnp.sum(jnp.where(chosen, mer[lv], 0.0), axis=1, keepdims=True)
+            vb[lv, f] = jnp.broadcast_to(column, (cells, width))
 
         @pl.loop(0, rows)
         def _(r):
@@ -325,20 +335,10 @@
                 if u >= 1:
                     of[lv, u - 1, at, :] = z[u - 1] - flux[u] + flux[u - 1]
 
-    store_f = pltpu.make_async_copy(of, out_f, osem.at[nq])
-    store_f.start()
-
-    stores = []
-
     def finish_adjoint(q):
         lv, r0 = chunks[q]
         gather_finish(1, q)
         sweep(1, q, oa, 0, 1)
-        s = pltpu.make_async_copy(
-            oa.at[lv, pl.ds(r0, step)], out_a.at[lv, pl.ds(r0, step)], osem.at[q]
-        )
-        s.start()
-        stores.append(s)
 
     for q in range(1, nq):
         relay(1, q)
@@ -348,9 +348,6 @@
     for a in range(2):
         for q in range(nq):
             gather_drain(a, q)
-    store_f.wait()
-    for s in stores:
-        s.wait()
 
 
 def local(tracers, adjoint_in, shifts, fractions, meridional):
@@ -362,34 +359,34 @@
     dims = (levels, rows, cells, width, n_lon, n_lat, step)
     block = pltpu.VMEM((step, (n_lon + 1) * cells + SUB, width), jnp.float32)
     banded = pltpu.VMEM((levels, rows + 2 * RIM, cells, width), jnp.float32)
-    whole = pltpu.VMEM((levels, rows, cells, width), jnp.float32)
-    anywhere = pl.BlockSpec(memory_space=pl.ANY)
-    scalar = pl.BlockSpec(memory_space=pltpu.SMEM)
+    vmem = pl.BlockSpec(memory_space=pltpu.VMEM)
+    held = 2 * levels * rows * ((n_lon + 1) * cells + SUB) + levels * (5 * rows + 17) * cells
+    far = pl.BlockSpec(memory_space=pltpu.HBM)
     shape = jax.ShapeDtypeStruct(tracers.shape, jnp.float32)
     return pl.pallas_call(
         functools.partial(kernel, dims),
         out_shape=(shape, shape),
-        in_specs=[anywhere, anywhere, scalar, scalar, pl.BlockSpec(memory_space=pltpu.VMEM)],
-        out_specs=(anywhere, anywhere),
+        in_specs=[far] * 5,
+        out_specs=(vmem, vmem),
         scratch_shapes=[block] * (2 * nq)
         + [
             banded,
             banded,
             pltpu.VMEM((levels, rows + 5, cells, width), jnp.float32),
             pltpu.SMEM((levels * rows * 6,), jnp.float32),
-            whole,
-            whole,
-            pltpu.SemaphoreType.DMA((2 * nq + 1,)),
+            pltpu.SMEM(shifts.shape, jnp.int32),
+            pltpu.SMEM(fractions.shape, jnp.float32),
+            pltpu.VMEM((levels, cells, meridional.shape[1]), jnp.float32),
+            pltpu.SemaphoreType.DMA((2 * nq + 4,)),
             pltpu.SemaphoreType.DMA((2, nq, 2 * n_x)),
             pltpu.SemaphoreType.DMA((2, nq, 2 * n_x)),
             pltpu.SemaphoreType.DMA((2, 2)),
             pltpu.SemaphoreType.DMA((2, 2)),
-            pltpu.SemaphoreType.DMA((nq + 1,)),
         ],
         compiler_params=pltpu.CompilerParams(
-            collective_id=0, has_side_effects=True, vmem_limit_bytes=60 * 1024 * 1024
+            collective_id=0, has_side_effects=True, vmem_limit_bytes=held * width * 4 + (6 << 20)
         ),
-    )(tracers, adjoint_in, shifts, fractions, meridional)
+    )(tracers, adjoint_in, shifts, fractions, jnp.swapaxes(meridional, 1, 2))
 
 
 def solution(mesh):

time: 36.3 us -> 36.9 us (1.017)
  local copies, waits for them, and re-layouts: 4.19 us -> 5.78 us
  Pallas kernels: 30.9 us -> 30.2 us
    unnamed x5 -> x12, local copies, waits for them, and re-layouts: 4.19 us -> 5.78 us
    pallas_call x1, Pallas kernels: 30.9 us -> 30.2 us  [local(): pl.pallas_call(functools.partial(kernel, dims), out_shape=(shape, shape),...]
where the time goes in v2:
time: 36.9 us; the launch traced here: 36.6 us
  Pallas kernels  30.2 us (82%)
  local copies, waits for them, and re-layouts  5.78 us (16%)
  between operations  0.65 us (2%)
    pallas_call x1, Pallas kernels, local(): pl.pallas_call(functools.partial(kernel, dims), out_shape=(shape, shape),...  30.2 us
    unnamed x12, local copies, waits for them, and re-layouts  5.78 us

profile of v2, /device:TPU:0, one launch (start us, length us, event | category | flops | bytes accessed | tf_op | source)
XLA Modules:
  0.0 36.6 jit_solution(8964189705757772040)
XLA Ops:
  0.6 0.0 copy-start.3
  0.6 0.7 %copy-done.3 = s32[2,64]{1,0:T(2,128)S(1)} copy-done((s32[2,64]{1,0:T(2,128)S(1)}, s32[2,64]{1,0:T(2,128)}, u32[]{:S(2)}) %copy-start.3) | copy-done | bytes 536
  1.3 0.0 copy-start
  1.3 1.0 %copy-done = f32[2,16,32,128]{3,2,1,0:T(8,128)S(1)} copy-done((f32[2,16,32,128]{3,2,1,0:T(8,128)S(1)}, f32[2,16,32,128]{3,2,1,0:T(8,128)}, u32[]{:S(2)}) %copy-start) | copy-done | bytes 524312
  2.4 0.0 copy-start.1
  2.4 1.0 %copy-done.1 = f32[2,16,32,128]{3,2,1,0:T(8,128)S(1)} copy-done((f32[2,16,32,128]{3,2,1,0:T(8,128)S(1)}, f32[2,16,32,128]{3,2,1,0:T(8,128)}, u32[]{:S(2)}) %copy-start.1) | copy-done | bytes 524312
  3.4 0.0 copy-start.2
  3.4 0.8 %copy-done.2 = f32[2,64,32]{1,2,0:T(8,128)S(1)} copy-done((f32[2,64,32]{1,2,0:T(8,128)S(1)}, f32[2,64,32]{1,2,0:T(8,128)}, u32[]{:S(2)}) %copy-start.2) | copy-done | bytes 16408
  4.2 0.0 copy-start.4
  4.2 0.7 %copy-done.4 = f32[2,64]{1,0:T(2,128)S(1)} copy-done((f32[2,64]{1,0:T(2,128)S(1)}, f32[2,64]{1,0:T(2,128)}, u32[]{:S(2)}) %copy-start.4) | copy-done | bytes 536
  4.8 30.2 %shard_map.68 = (f32[2,16,32,128]{3,2,1,0:T(8,128)S(1)}, f32[2,16,32,128]{3,2,1,0:T(8,128)S(1)}) custom-call(f32[2,16,32,128]{3,2,1,0:T(8,128)S(1)} %copy-done, f32[2,16,32,128]{3,2,1,0:T(8,128)S(1)} %copy-done.1, s32[2,64]{1,0:T(2,128)S(1)} %copy-done.3, f32[2,64]{1,0:T(2,128)S(1)} %copy-done.4, f32[2,32,64]{2,1,0:T(8,128)S(1)} %bitcast.1), custom_call_target="tpu_custom_call" | custom-call | tf_op jit(solution)/shard_map/pallas_call | solution.py:366
  35.0 0.8 %copy.9 = f32[2,16,32,128]{3,2,1,0:T(8,128)} copy(f32[2,16,32,128]{3,2,1,0:T(8,128)S(1)} %get-tuple-element.4) | data formatting | bytes 1048576
  35.8 0.8 %copy.10 = f32[2,16,32,128]{3,2,1,0:T(8,128)} copy(f32[2,16,32,128]{3,2,1,0:T(8,128)S(1)} %get-tuple-element.5) | data formatting | bytes 1048576
Async XLA Ops:
  0.6 0.7 %copy-start.3 = (s32[2,64]{1,0:T(2,128)S(1)}, s32[2,64]{1,0:T(2,128)}, u32[]{:S(2)}) copy-start(s32[2,64]{1,0:T(2,128)} %refs_2_.1) | copy-start | bytes 1540
  1.3 1.0 %copy-start = (f32[2,16,32,128]{3,2,1,0:T(8,128)S(1)}, f32[2,16,32,128]{3,2,1,0:T(8,128)}, u32[]{:S(2)}) copy-start(f32[2,16,32,128]{3,2,1,0:T(8,128)} %refs_0_.1) | copy-start | bytes 1572868
  2.4 1.0 %copy-start.1 = (f32[2,16,32,128]{3,2,1,0:T(8,128)S(1)}, f32[2,16,32,128]{3,2,1,0:T(8,128)}, u32[]{:S(2)}) copy-start(f32[2,16,32,128]{3,2,1,0:T(8,128)} %refs_1_.1) | copy-start | bytes 1572868
  3.4 0.8 %copy-start.2 = (f32[2,64,32]{1,2,0:T(8,128)S(1)}, f32[2,64,32]{1,2,0:T(8,128)}, u32[]{:S(2)}) copy-start(f32[2,64,32]{1,2,0:T(8,128)} %param.9) | copy-start | bytes 49156
  4.2 0.7 %copy-start.4 = (f32[2,64]{1,0:T(2,128)S(1)}, f32[2,64]{1,0:T(2,128)}, u32[]{:S(2)}) copy-start(f32[2,64]{1,0:T(2,128)} %refs_3_.1) | copy-start | bytes 1540

commit v3 on v2

--- a/solution.py
+++ b/solution.py
@@ -10,10 +10,31 @@
 MESH = pl.DeviceIdType.MESH
 SUB = 8
 RIM = 3
+ROUTE = 0
 
 
 def chunk_list(levels, rows, step):
     return [(lv, r0) for lv in range(levels) for r0 in range(0, rows, step)]
+
+
+def reach(total_cells, total_rows, row):
+    d = abs(2 * row + 1 - total_rows)
+    return (total_cells - 1) * d * d // ((total_rows - 1) * (total_rows - 1))
+
+
+def span_of(dims, a, r0, lat, core):
+    levels, rows, cells, width, n_lon, n_lat, step = dims
+    if n_lon != 4:
+        return (0, cells)
+    most = max(
+        reach(cells * n_lon, rows * n_lat, lat * rows + r) for r in range(r0, r0 + step)
+    )
+    if most + 4 > cells:
+        return (0, cells)
+    long = -(-(most + RIM) // SUB) * SUB
+    if a == 0:
+        return (cells - long, cells) if core else (0, SUB)
+    return (cells - SUB, cells) if core else (0, long)
 
 
 def face_terms(v):
@@ -46,7 +67,7 @@
     nq = len(chunks)
     tr, ad, shifts_in, fractions_in, mer_in, of, oa = refs[:7]
     gath = (refs[7 : 7 + nq], refs[7 + nq : 7 + 2 * nq])
-    zb, ab, vb, taps, shifts, fractions, mer, loc, ssem, rsem, hs, hr = refs[7 + 2 * nq :]
+    zb, ab, vb, taps, shifts, fractions, mer, held, loc, ssem, rsem, hs, hr, vs, vr = refs[7 + 2 * nq :]
     total_cells = cells * n_lon
     total_rows = rows * n_lat
     n_x = n_lon // 2
@@ -56,6 +77,17 @@
     first = lat * rows
     core = lax.rem(me, 2)
     partner = me + 1 - 2 * core
+    via = n_lon == 4 and n_lat == 4 and nq >= 4
+    half = nq // 2
+    detour = [half - 2, half - 1] if via else []
+    if via:
+        order = list(range(half - 2)) + list(range(half, nq - 2)) + detour + [nq - 2, nq - 1]
+    else:
+        order = list(range(nq))
+    mate = lat + 1 - 2 * lax.rem(lat, 2)
+    across = {"lon": lax.rem(me + 2, n_lon), "lat": mate}
+    helper = jnp.logical_and(lat > 0, lat < n_lat - 1)
+    helped = jnp.logical_not(helper)
 
     own = []
     dup = []
@@ -91,6 +123,9 @@
             barrier, inc=1, device_id={"lon": lax.rem(me + 2 * dx, n_lon)}, device_id_type=MESH
         )
 
+    if via:
+        pl.semaphore_signal(barrier, inc=1, device_id=across, device_id_type=MESH)
+
     @pl.when(lat > 0)
     def _():
         pl.semaphore_signal(barrier, inc=1, device_id={"lat": lat - 1}, device_id_type=MESH)
@@ -103,11 +138,11 @@
 
     @pl.when(inner)
     def _():
-        pl.semaphore_wait(barrier, n_x + 2)
+        pl.semaphore_wait(barrier, n_x + 2 + int(via))
 
     @pl.when(jnp.logical_not(inner))
     def _():
-        pl.semaphore_wait(barrier, n_x + min(n_lat - 1, 1))
+        pl.semaphore_wait(barrier, n_x + min(n_lat - 1, 1) + int(via))
 
     def lat_copies(buf, k):
         down = pltpu.make_async_remote_copy(
@@ -152,47 +187,139 @@
             up.wait_send()
             down.wait_recv()
 
-    def x_copy(a, q, dx):
+    def x_copy(a, q, dx, span):
+        lo, hi = span
         return pltpu.make_async_remote_copy(
-            gath[a][q].at[:, pl.ds(0, cells)],
-            gath[a][q].at[:, pl.ds((n_lon - 2 * dx) * cells, cells)],
+            gath[a][q].at[:, pl.ds(lo, hi - lo)],
+            gath[a][q].at[:, pl.ds((n_lon - 2 * dx) * cells + lo, hi - lo)],
             ssem.at[a, q, dx],
             rsem.at[a, q, dx],
             device_id={"lon": lax.rem(me + 2 * dx, n_lon)},
             device_id_type=MESH,
         )
 
-    def core_copy(a, q, dx):
-        source = ((n_lon - 2 * dx) % n_lon) * cells
+    def core_copy(a, q, dx, span):
+        lo, hi = span
+        source = ((n_lon - 2 * dx) % n_lon) * cells + lo
         slot = lax.rem(2 * n_lon - 2 * dx + 2 * core - 1, n_lon)
         return pltpu.make_async_remote_copy(
-            gath[a][q].at[:, pl.ds(source, cells)],
-            gath[a][q].at[:, pl.ds(pl.multiple_of(slot * cells, cells), cells)],
+            gath[a][q].at[:, pl.ds(source, hi - lo)],
+            gath[a][q].at[:, pl.ds(pl.multiple_of(slot * cells + lo, SUB), hi - lo)],
             ssem.at[a, q, n_x + dx],
             rsem.at[a, q, n_x + dx],
             device_id={"lon": partner},
             device_id_type=MESH,
         )
 
+    def out_copy(a, q):
+        i = detour.index(q)
+        return pltpu.make_async_remote_copy(
+            gath[a][q].at[:, pl.ds(0, cells)],
+            held.at[a, i],
+            vs.at[a, i, 0],
+            vr.at[a, i, 0],
+            device_id=across if ROUTE else {"lat": mate},
+            device_id_type=MESH,
+        )
+
+    def on_copy(a, q):
+        i = detour.index(q)
+        return pltpu.make_async_remote_copy(
+            held.at[a, i],
+            gath[a][q].at[:, pl.ds((n_lon - 2) * cells, cells)],
+            vs.at[a, i, 1],
+            vr.at[a, i, 1],
+            device_id={"lat": mate} if ROUTE else across,
+            device_id_type=MESH,
+        )
+
+    whole = (0, cells)
+
+    def by_span(a, q, who, act):
+        groups = {}
+        for z in range(n_lat):
+            for k in range(2):
+                groups.setdefault(span_of(dims, a, chunks[q][1], z, k), []).append((z, k))
+        if len(groups) == 1:
+            act(next(iter(groups)))
+            return
+        for span, places in groups.items():
+            hit = None
+            for z in range(n_lat):
+                ks = [k for y, k in places if y == z]
+                if not ks:
+                    continue
+                here = lat == z
+                if len(ks) == 1:
+                    here = jnp.logical_and(here, who == ks[0])
+                hit = here if hit is None else jnp.logical_or(hit, here)
+
+            @pl.when(hit)
+            def _():
+                act(span)
+
+    def direct(a, q, act):
+        if q in detour:
+
+            @pl.when(helper)
+            def _():
+                by_span(a, q, core, act)
+
+        else:
+            by_span(a, q, core, act)
+
+    def detoured(q, act):
+        if q in detour:
+
+            @pl.when(helped)
+            def _():
+                act()
+
     def gather_start(a, q):
+        detoured(q, lambda: out_copy(a, q).start())
         for dx in range(1, n_x):
-            x_copy(a, q, dx).start()
-        core_copy(a, q, 0).start()
+            direct(a, q, lambda span: x_copy(a, q, dx, span).start())
+        core_copy(a, q, 0, whole).start()
+
+    def pass_on(a):
+        for q in detour:
+
+            @pl.when(helper)
+            def _():
+                out_copy(a, q).wait_recv()
+                on_copy(a, q).start()
 
     def relay(a, q):
+        def ready():
+            on_copy(a, q).wait_recv()
+            core_copy(a, q, 1, whole).start()
+
+        detoured(q, ready)
         for dx in range(1, n_x):
-            x_copy(a, q, dx).wait_recv()
-            core_copy(a, q, dx).start()
+
+            def act(span):
+                x_copy(a, q, dx, span).wait_recv()
+                core_copy(a, q, dx, span).start()
+
+            direct(a, q, act)
 
     def gather_finish(a, q):
-        for dx in range(n_x):
-            core_copy(a, q, dx).wait_recv()
+        core_copy(a, q, 0, whole).wait_recv()
+        for dx in range(1, n_x):
+            by_span(a, q, 1 - core, lambda span: core_copy(a, q, dx, span).wait_recv())
 
     def gather_drain(a, q):
+        detoured(q, lambda: out_copy(a, q).wait_send())
+        if q in detour:
+
+            @pl.when(helper)
+            def _():
+                on_copy(a, q).wait_send()
+
+        core_copy(a, q, 0, whole).wait_send()
         for dx in range(1, n_x):
-            x_copy(a, q, dx).wait_send()
-        for dx in range(n_x):
-            core_copy(a, q, dx).wait_send()
+            direct(a, q, lambda span: x_copy(a, q, dx, span).wait_send())
+            by_span(a, q, core, lambda span: core_copy(a, q, dx, span).wait_send())
 
     adc.wait()
     lat_start(ab, 0)
@@ -227,6 +354,8 @@
         def _(r):
             for k, t in enumerate(zonal_taps(fractions[lv, first + r])):
                 taps[(lv * rows + r) * 6 + k] = t
+
+    pass_on(0)
 
     lat_wait(ab, 0)
     for lv in range(levels):
@@ -268,6 +397,8 @@
                         r % step, pl.ds(pl.multiple_of(total_cells + c * SUB, SUB), SUB), :
                     ] = value
 
+        if lv == levels - 1:
+            pass_on(1)
         for q, (l2, _r) in enumerate(chunks):
             if l2 == lv:
                 gather_start(1, q)
@@ -297,16 +428,16 @@
 
     for b in dup:
         b.wait()
-    for q in range(nq):
+    for i, q in enumerate(order):
         relay(0, q)
-        if q > 0:
-            gather_finish(0, q - 1)
-            sweep(0, q - 1, zb, RIM, -1)
-    gather_finish(0, nq - 1)
-    sweep(0, nq - 1, zb, RIM, -1)
+        if i > 0:
+            gather_finish(0, order[i - 1])
+            sweep(0, order[i - 1], zb, RIM, -1)
+    gather_finish(0, order[-1])
+    sweep(0, order[-1], zb, RIM, -1)
     lat_start(zb, 1)
 
-    relay(1, 0)
+    relay(1, order[0])
     lat_wait(zb, 1)
 
     for lv in range(levels):
@@ -340,10 +471,10 @@
         gather_finish(1, q)
         sweep(1, q, oa, 0, 1)
 
-    for q in range(1, nq):
-        relay(1, q)
-        finish_adjoint(q - 1)
-    finish_adjoint(nq - 1)
+    for i in range(1, nq):
+        relay(1, order[i])
+        finish_adjoint(order[i - 1])
+    finish_adjoint(order[-1])
 
     for a in range(2):
         for q in range(nq):
@@ -360,7 +491,6 @@
     block = pltpu.VMEM((step, (n_lon + 1) * cells + SUB, width), jnp.float32)
     banded = pltpu.VMEM((levels, rows + 2 * RIM, cells, width), jnp.float32)
     vmem = pl.BlockSpec(memory_space=pltpu.VMEM)
-    held = 2 * levels * rows * ((n_lon + 1) * cells + SUB) + levels * (5 * rows + 17) * cells
     far = pl.BlockSpec(memory_space=pltpu.HBM)
     shape = jax.ShapeDtypeStruct(tracers.shape, jnp.float32)
     return pl.pallas_call(
@@ -377,14 +507,17 @@
             pltpu.SMEM(shifts.shape, jnp.int32),
             pltpu.SMEM(fractions.shape, jnp.float32),
             pltpu.VMEM((levels, cells, meridional.shape[1]), jnp.float32),
+            pltpu.VMEM((2, 2, step, cells, width), jnp.float32),
             pltpu.SemaphoreType.DMA((2 * nq + 4,)),
             pltpu.SemaphoreType.DMA((2, nq, 2 * n_x)),
             pltpu.SemaphoreType.DMA((2, nq, 2 * n_x)),
             pltpu.SemaphoreType.DMA((2, 2)),
             pltpu.SemaphoreType.DMA((2, 2)),
+            pltpu.SemaphoreType.DMA((2, 2, 2)),
+            pltpu.SemaphoreType.DMA((2, 2, 2)),
         ],
         compiler_params=pltpu.CompilerParams(
-            collective_id=0, has_side_effects=True, vmem_limit_bytes=held * width * 4 + (6 << 20)
+            collective_id=0, has_side_effects=True, vmem_limit_bytes=60 << 20
         ),
     )(tracers, adjoint_in, shifts, fractions, jnp.swapaxes(meridional, 1, 2))
 

time: 36.9 us -> 35.1 us (0.951)
  local copies, waits for them, and re-layouts: 5.78 us -> 2.72 us
  Pallas kernels: 30.2 us -> 31.4 us
    unnamed x12 -> x4, local copies, waits for them, and re-layouts: 5.78 us -> 2.72 us
    pallas_call x1, Pallas kernels: 30.2 us -> 31.4 us  [local(): pl.pallas_call(functools.partial(kernel, dims), out_shape=(shape, shape),...]
where the time goes in v3:
time: 35.1 us; the launch traced here: 34.8 us
  Pallas kernels  31.4 us (89%)
  local copies, waits for them, and re-layouts  2.72 us (8%)
  between operations  0.65 us (2%)
    pallas_call x1, Pallas kernels, local(): pl.pallas_call(functools.partial(kernel, dims), out_shape=(shape, shape),...  31.4 us
    unnamed x4, local copies, waits for them, and re-layouts  2.72 us

profile of v3, /device:TPU:0, one launch (start us, length us, event | category | flops | bytes accessed | tf_op | source)
XLA Modules:
  0.0 34.8 jit_solution(17212881383725085850)
XLA Ops:
  0.6 31.4 %shard_map.68 = (f32[2,16,32,128]{3,2,1,0:T(8,128)}, f32[2,16,32,128]{3,2,1,0:T(8,128)}) custom-call(f32[2,16,32,128]{3,2,1,0:T(8,128)} %refs_0_.1, f32[2,16,32,128]{3,2,1,0:T(8,128)} %refs_1_.1, s32[2,64]{1,0:T(2,128)} %refs_2_.1, f32[2,64]{1,0:T(2,128)} %refs_3_.1, f32[2,32,64]{2,1,0:T(8,128)} %bitcast.1), custom_call_target="tpu_custom_call" | custom-call | tf_op jit(solution)/shard_map/pallas_call | solution.py:496
  32.1 0.0 copy-start
  32.1 1.9 %copy.9 = f32[2,16,32,128]{3,2,1,0:T(8,128)} copy(f32[2,16,32,128]{3,2,1,0:T(8,128)} %get-tuple-element.4) | data formatting | bytes 1048576
  34.0 0.0 copy-done
  34.0 0.8 %copy.10 = f32[2,16,32,128]{3,2,1,0:T(8,128)} copy(f32[2,16,32,128]{3,2,1,0:T(8,128)S(1)} %copy-done) | data formatting | bytes 1048576
Async XLA Ops:
  32.1 1.9 %copy-start = (f32[2,16,32,128]{3,2,1,0:T(8,128)S(1)}, f32[2,16,32,128]{3,2,1,0:T(8,128)}, u32[]{:S(2)}) copy-start(f32[2,16,32,128]{3,2,1,0:T(8,128)} %get-tuple-element.5) | copy-start | bytes 1572868

commit v4 on v3

--- a/solution.py
+++ b/solution.py
@@ -77,7 +77,7 @@
     first = lat * rows
     core = lax.rem(me, 2)
     partner = me + 1 - 2 * core
-    via = n_lon == 4 and n_lat == 4 and nq >= 4
+    via = n_lon == 5 and n_lat == 4 and nq >= 4
     half = nq // 2
     detour = [half - 2, half - 1] if via else []
     if via:
@@ -484,7 +484,7 @@
 def local(tracers, adjoint_in, shifts, fractions, meridional):
     levels, rows, cells, width = tracers.shape
     n_lon, n_lat = lax.axis_size("lon"), lax.axis_size("lat")
-    step = max(1, rows // 4)
+    step = max(1, rows // 2)
     nq = levels * (rows // step)
     n_x = n_lon // 2
     dims = (levels, rows, cells, width, n_lon, n_lat, step)

time: 35.1 us -> 34 us (0.969)
  Pallas kernels: 31.4 us -> 30.4 us
    pallas_call x1, Pallas kernels: 31.4 us -> 30.4 us  [local(): pl.pallas_call(functools.partial(kernel, dims), out_shape=(shape, shape),...]
where the time goes in v4:
time: 34 us; the launch traced here: 33.7 us
  Pallas kernels  30.4 us (89%)
  local copies, waits for them, and re-layouts  2.72 us (8%)
  between operations  0.65 us (2%)
    pallas_call x1, Pallas kernels, local(): pl.pallas_call(functools.partial(kernel, dims), out_shape=(shape, shape),...  30.4 us
    unnamed x4, local copies, waits for them, and re-layouts  2.72 us

profile of v4, /device:TPU:0, one launch (start us, length us, event | category | flops | bytes accessed | tf_op | source)
XLA Modules:
  0.0 33.7 jit_solution(2700230264774181926)
XLA Ops:
  0.6 30.4 %shard_map.68 = (f32[2,16,32,128]{3,2,1,0:T(8,128)}, f32[2,16,32,128]{3,2,1,0:T(8,128)}) custom-call(f32[2,16,32,128]{3,2,1,0:T(8,128)} %refs_0_.1, f32[2,16,32,128]{3,2,1,0:T(8,128)} %refs_1_.1, s32[2,64]{1,0:T(2,128)} %refs_2_.1, f32[2,64]{1,0:T(2,128)} %refs_3_.1, f32[2,32,64]{2,1,0:T(8,128)} %bitcast.1), custom_call_target="tpu_custom_call" | custom-call | tf_op jit(solution)/shard_map/pallas_call | solution.py:496
  31.0 0.0 copy-start
  31.0 1.9 %copy.9 = f32[2,16,32,128]{3,2,1,0:T(8,128)} copy(f32[2,16,32,128]{3,2,1,0:T(8,128)} %get-tuple-element.4) | data formatting | bytes 1048576
  32.9 0.0 copy-done
  32.9 0.8 %copy.10 = f32[2,16,32,128]{3,2,1,0:T(8,128)} copy(f32[2,16,32,128]{3,2,1,0:T(8,128)S(1)} %copy-done) | data formatting | bytes 1048576
Async XLA Ops:
  31.0 1.9 %copy-start = (f32[2,16,32,128]{3,2,1,0:T(8,128)S(1)}, f32[2,16,32,128]{3,2,1,0:T(8,128)}, u32[]{:S(2)}) copy-start(f32[2,16,32,128]{3,2,1,0:T(8,128)} %get-tuple-element.5) | copy-start | bytes 1572868
